TPU v7x, 32 devices: a whole 2x2x4 slice. The times are simulated.
32 devices in a mesh: lat: 4 (over y, core), lon: 8 (over z, x).
Axes of the slice: x: 2, y: 2, z: 4, core: 2. Of those that a mesh axis runs over, the one named last changes fastest.
Arguments:
- field: float32 [64, 1024, 128], P('lon', 'lat'), may hold values from -6 to 6
- kappa: float32 [64, 1024], P('lon', 'lat'), may hold values from 0.06 to 0.24
- classes: int32 [64, 1024], P('lon', 'lat'), may hold values from 0 to 7
- inverses: float32 [8, 128, 128], replicated, as said below
Outputs:
- result: float32 [64, 1024, 128], P('lon', 'lat')
Inputs may be any that keep to these rules, and one draw needn't show every extreme that they name: `inverses`: each matrix has diagonal entries between 0.4 and 1.0 and dense, full-rank off-diagonal entries of magnitude about 0.02; the matrices are not diagonally dominant.
All inputs are finite; a program needn't handle non-finite values.
Results may differ from a plain program's by a relative error of at most 0.00013.
Values sent between devices are 32-bit elements; how exact they have to be, the bound alone decides.
A program may use at most 64 MiB of HBM per device.

v0:
```python
import jax
import jax.numpy as jnp
from jax import lax
from jax.sharding import PartitionSpec as P

STEPS = 6


def with_halo(array, sides, width, wrap):
    for axis, dim in sides:
        size, length = (lax.axis_size(axis), array.shape[dim])
        up = [(i, (i + 1) % size) for i in range(size if wrap else size - 1)]
        down = [(j, i) for i, j in up]
        last = lax.slice_in_dim(array, length - width, length, axis=dim)
        initial = lax.slice_in_dim(array, 0, width, axis=dim)
        before = lax.ppermute(last, axis, up)
        after = lax.ppermute(initial, axis, down)
        array = jnp.concatenate([before, array, after], axis=dim)
    return array


def widen(values, width):
    values = with_halo(values, (("lon", 0),), width, True)
    return with_halo(values, (("lat", 1),), width, False)


def widen_kinds(values, width):
    values = with_halo(values, (("lon", 0),), width, True)
    return with_halo(values, (("lat", 1),), width, False)


def trim(values, margin):
    if margin == 0:
        return values
    return values[margin : values.shape[0] - margin, margin : values.shape[1] - margin]


def explicit(extended, k_ext):
    centre = extended[1:-1, 1:-1]
    k_centre = k_ext[1:-1, 1:-1]
    total = (0.5 * (k_centre + k_ext[2:, 1:-1]))[..., None] * (extended[2:, 1:-1] - centre)
    total = total + (0.5 * (k_centre + k_ext[:-2, 1:-1]))[..., None] * (
        extended[:-2, 1:-1] - centre
    )
    total = total + (0.5 * (k_centre + k_ext[1:-1, 2:]))[..., None] * (extended[1:-1, 2:] - centre)
    total = total + (0.5 * (k_centre + k_ext[1:-1, :-2]))[..., None] * (
        extended[1:-1, :-2] - centre
    )
    return centre + total


def vertical(values, kinds, inverses):
    picker = (kinds[..., None] == jnp.arange(inverses.shape[0], dtype=jnp.int32)).astype(
        jnp.float32
    )
    every = jnp.einsum("xyl,kml->xykm", values, inverses, precision=lax.Precision.HIGHEST)
    return jnp.sum(picker[..., None] * every, axis=2)


def body(field, kappa, classes, inverses):
    state = field
    depth = 3
    lat_rows = kappa.shape[1]
    k_ext = widen(kappa, depth)
    kinds_ext = widen_kinds(classes, depth)
    rows = (
        lax.axis_index("lat") * lat_rows - depth + jnp.arange(lat_rows + 2 * depth, dtype=jnp.int32)
    )
    inside = ((rows >= 0) & (rows < lat_rows * lax.axis_size("lat"))).astype(jnp.float32)
    for group in range(STEPS // depth):
        extended = widen(state, depth)
        for inner in range(depth):
            margin = depth - inner
            fresh = explicit(extended, trim(k_ext, depth - margin))
            cut = depth - margin + 1
            keep = inside[cut : inside.shape[0] - cut]
            fresh = fresh * keep[None, :, None]
            extended = vertical(fresh, trim(kinds_ext, cut), inverses)
        state = extended
    return state


def solution(mesh):
    return jax.shard_map(
        body,
        mesh=mesh,
        in_specs=(P("lon", "lat", None), P("lon", "lat"), P("lon", "lat"), P()),
        out_specs=P("lon", "lat", None),
        check_vma=False,
    )
```

profile of v0, /device:TPU:3, one launch (start us, length us, event | category | flops | bytes accessed | tf_op | source)
XLA Modules:
  0.0 133.3 jit_solution(4305158363567170042)
XLA Ops:
  0.0 0.8 fusion.152
  0.8 1.3 collective-permute-start.8
  2.1 0.2 collective-permute-start.9
  2.3 0.8 fusion.153
  3.1 2.2 %collective-permute-start = (s32[3,256]{1,0:T(4,128)S(1)}, s32[3,256]{1,0:T(4,128)S(1)}, u32[]{:S(2)}, u32[]{:S(2)}) collective-permute-start(s32[3,256]{1,0:T(4,128)S(1)} %get-tuple-element.33), channel_id=1, source_target_pairs={{0,1},{1,2},{2,3},{3,4},{4,5},{5,6},{6,7},{7,0},{8,9},{9,10},{10,1... | collective-permute-start | bytes 9224 | tf_op jit(solution)/shard_map/ppermute | solution.py:16
  5.2 0.9 collective-permute-start.1
  6.2 1.2 fusion.149
  7.3 1.5 %collective-permute-start.4 = (f32[3,256,128]{2,1,0:T(8,128)S(1)}, f32[3,256,128]{2,1,0:T(8,128)S(1)}, u32[]{:S(2)}, u32[]{:S(2)}) collective-permute-start(f32[3,256,128]{2,1,0:T(8,128)S(1)} %get-tuple-element.12), channel_id=1, source_target_pairs={{0,1},{1,2},{2,3},{3,4},{4,5},{5,6},{6,7},{7,0},{8,9},{9,10},{10,1... | collective-permute-start | bytes 1179656 | tf_op jit(solution)/shard_map/ppermute | solution.py:16
  8.8 0.1 slice.263
  8.9 0.1 slice.274
  9.0 0.1 slice.284
  9.1 2.7 %collective-permute-start.5 = (f32[3,256,128]{2,1,0:T(8,128)S(1)}, f32[3,256,128]{2,1,0:T(8,128)S(1)}, u32[]{:S(2)}, u32[]{:S(2)}) collective-permute-start(f32[3,256,128]{2,1,0:T(8,128)S(1)} %get-tuple-element.11), channel_id=1, source_target_pairs={{1,0},{2,1},{3,2},{4,3},{5,4},{6,5},{7,6},{0,7},{9,8},{10,9},{11,1... | collective-permute-start | bytes 1179656 | tf_op jit(solution)/shard_map/ppermute | solution.py:17
  11.8 0.1 fusion.150
  11.9 0.1 fusion.151
  12.0 5.0 %collective-permute-start.2 = (s32[14,3]{1,0:T(8,128)S(1)}, s32[14,3]{1,0:T(8,128)S(1)}, u32[]{:S(2)}, u32[]{:S(2)}) collective-permute-start(s32[14,3]{1,0:T(8,128)S(1)} %get-tuple-element.27), channel_id=1, source_target_pairs={{0,8},{8,16},{16,24},{1,9},{9,17},{17,25},{2,10},{10,18},{18,26},{... | collective-permute-start | bytes 512 | tf_op jit(solution)/shard_map/ppermute | solution.py:16
  17.0 1.9 %collective-permute-start.10 = (f32[14,3]{1,0:T(8,128)S(1)}, f32[14,3]{1,0:T(8,128)S(1)}, u32[]{:S(2)}, u32[]{:S(2)}) collective-permute-start(f32[14,3]{1,0:T(8,128)S(1)} %get-tuple-element.25), channel_id=1, source_target_pairs={{0,8},{8,16},{16,24},{1,9},{9,17},{17,25},{2,10},{10,18},{18,26},{... | collective-permute-start | bytes 512 | tf_op jit(solution)/shard_map/ppermute | solution.py:16
  18.9 2.4 %collective-permute-start.3 = (s32[14,3]{1,0:T(8,128)S(1)}, s32[14,3]{1,0:T(8,128)S(1)}, u32[]{:S(2)}, u32[]{:S(2)}) collective-permute-start(s32[14,3]{1,0:T(8,128)S(1)} %get-tuple-element.28), channel_id=1, source_target_pairs={{8,0},{16,8},{24,16},{9,1},{17,9},{25,17},{10,2},{18,10},{26,18},{... | collective-permute-start | bytes 512 | tf_op jit(solution)/shard_map/ppermute | solution.py:17
  21.3 1.9 %collective-permute-start.11 = (f32[14,3]{1,0:T(8,128)S(1)}, f32[14,3]{1,0:T(8,128)S(1)}, u32[]{:S(2)}, u32[]{:S(2)}) collective-permute-start(f32[14,3]{1,0:T(8,128)S(1)} %get-tuple-element.26), channel_id=1, source_target_pairs={{8,0},{16,8},{24,16},{9,1},{17,9},{25,17},{10,2},{18,10},{26,18},{... | collective-permute-start | bytes 512 | tf_op jit(solution)/shard_map/ppermute | solution.py:17
  23.2 0.9 collective-permute-done.3
  24.2 0.1 pad_add_fusion
  24.2 0.1 slice.307
  24.3 0.1 slice.306
  24.4 2.2 %collective-permute-done.11 = f32[14,3]{1,0:T(8,128)S(1)} collective-permute-done((f32[14,3]{1,0:T(8,128)S(1)}, f32[14,3]{1,0:T(8,128)S(1)}, u32[]{:S(2)}, u32[]{:S(2)}) %collective-permute-start.11) | collective-permute-done | bytes 200 | tf_op jit(solution)/shard_map/ppermute | solution.py:17
  26.6 0.1 pad_maximum_fusion.5
  26.7 0.1 pad_maximum_fusion.6
  26.7 0.1 fusion.132
  26.9 0.1 fusion.136
  27.0 2.5 %collective-permute-done.4 = f32[3,256,128]{2,1,0:T(8,128)S(1)} collective-permute-done((f32[3,256,128]{2,1,0:T(8,128)S(1)}, f32[3,256,128]{2,1,0:T(8,128)S(1)}, u32[]{:S(2)}, u32[]{:S(2)}) %collective-permute-start.4) | collective-permute-done | bytes 393248 | tf_op jit(solution)/shard_map/ppermute | solution.py:16
  29.5 0.1 constant_dynamic-update-slice_fusion.1
  29.6 3.5 %collective-permute-start.6 = (f32[14,3,128]{2,1,0:T(4,128)S(1)}, f32[14,3,128]{2,1,0:T(4,128)S(1)}, u32[]{:S(2)}, u32[]{:S(2)}) collective-permute-start(f32[14,3,128]{2,1,0:T(4,128)S(1)} %get-tuple-element.7), channel_id=1, source_target_pairs={{0,8},{8,16},{16,24},{1,9},{9,17},{17,25},{2,10},{10,18},{18,26},{... | collective-permute-start | bytes 64520 | tf_op jit(solution)/shard_map/ppermute | solution.py:16
  33.2 1.9 %collective-permute-start.7 = (f32[14,3,128]{2,1,0:T(4,128)S(1)}, f32[14,3,128]{2,1,0:T(4,128)S(1)}, u32[]{:S(2)}, u32[]{:S(2)}) collective-permute-start(f32[14,3,128]{2,1,0:T(4,128)S(1)} %get-tuple-element.8), channel_id=1, source_target_pairs={{8,0},{16,8},{24,16},{9,1},{17,9},{25,17},{10,2},{18,10},{26,18},{... | collective-permute-start | bytes 64520 | tf_op jit(solution)/shard_map/ppermute | solution.py:17
  35.1 0.1 fusion.138
  35.2 3.2 %collective-permute-done.7 = f32[14,3,128]{2,1,0:T(4,128)S(1)} collective-permute-done((f32[14,3,128]{2,1,0:T(4,128)S(1)}, f32[14,3,128]{2,1,0:T(4,128)S(1)}, u32[]{:S(2)}, u32[]{:S(2)}) %collective-permute-start.7) | collective-permute-done | bytes 21536 | tf_op jit(solution)/shard_map/ppermute | solution.py:17
  38.3 0.1 pad_maximum_fusion
  38.5 14.1 %multiply_reduce_fusion.1 = f32[12,260,128]{2,1,0:T(8,128)S(1)} fusion(f32[12,260,8]{1,2,0:T(8,128)S(1)} %fusion.126, f32[14,262,128]{2,1,0:T(8,128)S(1)} %pad_maximum_fusion, f32[260]{0:T(512)S(1)} %slice.263, f32[12,260]{1,0:T(8,128)S(1)} %get-tuple-element.18, f32[12,260]{1,0:T(8,128)S(1)} %get-tuple-element.19, f32[12,260]{1,0:T(8,128)S(1)} %get-tuple-element.20, ...), kind=kOutput, calls=%fused_computation.1 | convolution fusion | flops 4918517760 | bytes 10479616 | tf_op jit(solution)/shard_map/xyl,kml->xykm/dot_general | solution.py:56
  52.6 11.6 %multiply_reduce_fusion.3 = f32[10,258,128]{2,1,0:T(8,128)S(1)} fusion(f32[10,258,8]{1,2,0:T(8,128)S(1)} %fusion.127, f32[12,260,128]{2,1,0:T(8,128)S(1)} %multiply_reduce_fusion.1, f32[258]{0:T(512)S(1)} %slice.274, f32[10,258]{1,0:T(8,128)S(1)} %get-tuple-element.16, f32[10,258]{1,0:T(8,128)S(1)} %get-tuple-element.15, ...), kind=kOutput, calls=%fused_computation.3 | convolution fusion | flops 4067235840 | bytes 8826880 | tf_op jit(solution)/shard_map/xyl,kml->xykm/dot_general | solution.py:56
  64.2 8.7 %multiply_reduce_fusion.5 = f32[8,256,128]{2,1,0:T(8,128)S(1)} fusion(f32[8,256,8]{1,2,0:T(8,128)S(1)} %fusion.128, f32[10,258,128]{2,1,0:T(8,128)S(1)} %multiply_reduce_fusion.3, f32[8,128,128]{2,1,0:T(8,128)S(1)} %copy-done, f32[256]{0:T(256)S(1)} %slice.284, f32[8,256]{1,0:T(8,128)S(1)} %get-tuple-element.22, f32[8,256]{1,0:T(8,128)S(1)} %get-tuple-element.21, ...), kind=kOutput, calls=%fused_computation.5 | convolution fusion | flops 3228565504 | bytes 6915072 | tf_op jit(solution)/shard_map/xyl,kml->xykm/dot_general | solution.py:56
  72.9 0.1 fusion.148
  72.9 0.1 collective-permute-start.12
  73.0 1.7 %collective-permute-start.13 = (f32[3,256,128]{2,1,0:T(8,128)S(1)}, f32[3,256,128]{2,1,0:T(8,128)S(1)}, u32[]{:S(2)}, u32[]{:S(2)}) collective-permute-start(f32[3,256,128]{2,1,0:T(8,128)S(1)} %get-tuple-element.10), channel_id=1, source_target_pairs={{1,0},{2,1},{3,2},{4,3},{5,4},{6,5},{7,6},{0,7},{9,8},{10,9},{11,1... | collective-permute-start | bytes 1179656 | tf_op jit(solution)/shard_map/ppermute | solution.py:17
  74.7 15.9 %collective-permute-done.12 = f32[3,256,128]{2,1,0:T(8,128)S(1)} collective-permute-done((f32[3,256,128]{2,1,0:T(8,128)S(1)}, f32[3,256,128]{2,1,0:T(8,128)S(1)}, u32[]{:S(2)}, u32[]{:S(2)}) %collective-permute-start.12) | collective-permute-done | bytes 393248 | tf_op jit(solution)/shard_map/ppermute | solution.py:16
  90.6 2.0 %collective-permute-start.14 = (f32[14,3,128]{2,1,0:T(4,128)S(1)}, f32[14,3,128]{2,1,0:T(4,128)S(1)}, u32[]{:S(2)}, u32[]{:S(2)}) collective-permute-start(f32[14,3,128]{2,1,0:T(4,128)S(1)} %get-tuple-element.5), channel_id=1, source_target_pairs={{0,8},{8,16},{16,24},{1,9},{9,17},{17,25},{2,10},{10,18},{18,26},{... | collective-permute-start | bytes 64520 | tf_op jit(solution)/shard_map/ppermute | solution.py:16
  92.6 2.5 %collective-permute-start.15 = (f32[14,3,128]{2,1,0:T(4,128)S(1)}, f32[14,3,128]{2,1,0:T(4,128)S(1)}, u32[]{:S(2)}, u32[]{:S(2)}) collective-permute-start(f32[14,3,128]{2,1,0:T(4,128)S(1)} %get-tuple-element.6), channel_id=1, source_target_pairs={{8,0},{16,8},{24,16},{9,1},{17,9},{25,17},{10,2},{18,10},{26,18},{... | collective-permute-start | bytes 64520 | tf_op jit(solution)/shard_map/ppermute | solution.py:17
  95.2 2.7 %collective-permute-done.15 = f32[14,3,128]{2,1,0:T(4,128)S(1)} collective-permute-done((f32[14,3,128]{2,1,0:T(4,128)S(1)}, f32[14,3,128]{2,1,0:T(4,128)S(1)}, u32[]{:S(2)}, u32[]{:S(2)}) %collective-permute-start.15) | collective-permute-done | bytes 21536 | tf_op jit(solution)/shard_map/ppermute | solution.py:17
  97.8 0.1 pad_maximum_fusion.1
  98.0 14.1 %multiply_reduce_fusion = f32[12,260,128]{2,1,0:T(8,128)S(1)} fusion(f32[12,260,8]{1,2,0:T(8,128)S(1)} %fusion.126, f32[14,262,128]{2,1,0:T(8,128)S(1)} %pad_maximum_fusion.1, f32[260]{0:T(512)S(1)} %slice.263, f32[12,260]{1,0:T(8,128)S(1)} %get-tuple-element.18, f32[12,260]{1,0:T(8,128)S(1)} %get-tuple-element.19, f32[12,260]{1,0:T(8,128)S(1)} %get-tuple-element.20, ...), kind=kOutput, calls=%fused_computation | convolution fusion | flops 4918517760 | bytes 10479616 | tf_op jit(solution)/shard_map/xyl,kml->xykm/dot_general | solution.py:56
  112.1 11.6 %multiply_reduce_fusion.2 = f32[10,258,128]{2,1,0:T(8,128)S(1)} fusion(f32[10,258,8]{1,2,0:T(8,128)S(1)} %fusion.127, f32[12,260,128]{2,1,0:T(8,128)S(1)} %multiply_reduce_fusion, f32[258]{0:T(512)S(1)} %slice.274, f32[10,258]{1,0:T(8,128)S(1)} %get-tuple-element.16, f32[10,258]{1,0:T(8,128)S(1)} %get-tuple-element.15, f32[10,258]{1,0:T(8,128)S(1)} %get-tuple-element.14, ...), kind=kOutput, calls=%fused_computation.2 | convolution fusion | flops 4067235840 | bytes 8826880 | tf_op jit(solution)/shard_map/xyl,kml->xykm/dot_general | solution.py:56
  123.7 9.6 %multiply_reduce_fusion.4 = f32[8,256,128]{2,1,0:T(8,128)} fusion(f32[8,256,8]{1,2,0:T(8,128)S(1)} %fusion.128, f32[10,258,128]{2,1,0:T(8,128)S(1)} %multiply_reduce_fusion.2, f32[8,128,128]{2,1,0:T(8,128)S(1)} %copy-done, f32[256]{0:T(256)S(1)} %slice.284, f32[8,256]{1,0:T(8,128)S(1)} %get-tuple-element.22, f32[8,256]{1,0:T(8,128)S(1)} %get-tuple-element.21, ...), kind=kOutput, calls=%fused_computation.4 | convolution fusion | flops 3228565504 | bytes 6915072 | tf_op jit(solution)/shard_map/xyl,kml->xykm/dot_general | solution.py:56
  (28 shorter events, 0.2 us)
Async XLA Ops:
  0.0 38.5 %copy-start = (f32[8,128,128]{2,1,0:T(8,128)S(1)}, f32[8,128,128]{2,1,0:T(8,128)}, u32[]{:S(2)}) copy-start(f32[8,128,128]{2,1,0:T(8,128)} %param.7) | copy-start | bytes 1572868
  0.0 11.8 %copy-start.2 = (f32[8,256]{1,0:T(8,128)S(1)}, f32[8,256]{1,0:T(8,128)}, u32[]{:S(2)}) copy-start(f32[8,256]{1,0:T(8,128)} %param.5) | copy-start | bytes 24580
  0.0 8.8 %copy-start.3 = (s32[8,256]{1,0:T(8,128)S(1)}, s32[8,256]{1,0:T(8,128)}, u32[]{:S(2)}) copy-start(s32[8,256]{1,0:T(8,128)} %param.6) | copy-start | bytes 24580
  0.8 8.2 %collective-permute-start.8 = (f32[3,256]{1,0:T(4,128)S(1)}, f32[3,256]{1,0:T(4,128)S(1)}, u32[]{:S(2)}, u32[]{:S(2)}) collective-permute-start(f32[3,256]{1,0:T(4,128)S(1)} %get-tuple-element.31), channel_id=1, source_target_pairs={{0,1},{1,2},{2,3},{3,4},{4,5},{5,6},{6,7},{7,0},{8,9},{9,10},{10,1... | collective-permute-start | bytes 9224 | tf_op jit(solution)/shard_map/ppermute | solution.py:16
  2.1 9.7 %collective-permute-start.9 = (f32[3,256]{1,0:T(4,128)S(1)}, f32[3,256]{1,0:T(4,128)S(1)}, u32[]{:S(2)}, u32[]{:S(2)}) collective-permute-start(f32[3,256]{1,0:T(4,128)S(1)} %get-tuple-element.32), channel_id=1, source_target_pairs={{1,0},{2,1},{3,2},{4,3},{5,4},{6,5},{7,6},{0,7},{9,8},{10,9},{11,1... | collective-permute-start | bytes 9224 | tf_op jit(solution)/shard_map/ppermute | solution.py:17
  3.1 8.8 %collective-permute-start = (s32[3,256]{1,0:T(4,128)S(1)}, s32[3,256]{1,0:T(4,128)S(1)}, u32[]{:S(2)}, u32[]{:S(2)}) collective-permute-start(s32[3,256]{1,0:T(4,128)S(1)} %get-tuple-element.33), channel_id=1, source_target_pairs={{0,1},{1,2},{2,3},{3,4},{4,5},{5,6},{6,7},{7,0},{8,9},{9,10},{10,1... | collective-permute-start | bytes 9224 | tf_op jit(solution)/shard_map/ppermute | solution.py:16
  5.2 24.2 %copy-start.1 = (f32[8,256,128]{2,1,0:T(8,128)S(1)}, f32[8,256,128]{2,1,0:T(8,128)}, u32[]{:S(2)}) copy-start(f32[8,256,128]{2,1,0:T(8,128)} %param.4) | copy-start | bytes 3145732
  5.2 6.6 %collective-permute-start.1 = (s32[3,256]{1,0:T(4,128)S(1)}, s32[3,256]{1,0:T(4,128)S(1)}, u32[]{:S(2)}, u32[]{:S(2)}) collective-permute-start(s32[3,256]{1,0:T(4,128)S(1)} %get-tuple-element.34), channel_id=1, source_target_pairs={{1,0},{2,1},{3,2},{4,3},{5,4},{6,5},{7,6},{0,7},{9,8},{10,9},{11,1... | collective-permute-start | bytes 9224 | tf_op jit(solution)/shard_map/ppermute | solution.py:17
  7.3 22.1 %collective-permute-start.4 = (f32[3,256,128]{2,1,0:T(8,128)S(1)}, f32[3,256,128]{2,1,0:T(8,128)S(1)}, u32[]{:S(2)}, u32[]{:S(2)}) collective-permute-start(f32[3,256,128]{2,1,0:T(8,128)S(1)} %get-tuple-element.12), channel_id=1, source_target_pairs={{0,1},{1,2},{2,3},{3,4},{4,5},{5,6},{6,7},{7,0},{8,9},{9,10},{10,1... | collective-permute-start | bytes 1179656 | tf_op jit(solution)/shard_map/ppermute | solution.py:16
  9.1 20.5 %collective-permute-start.5 = (f32[3,256,128]{2,1,0:T(8,128)S(1)}, f32[3,256,128]{2,1,0:T(8,128)S(1)}, u32[]{:S(2)}, u32[]{:S(2)}) collective-permute-start(f32[3,256,128]{2,1,0:T(8,128)S(1)} %get-tuple-element.11), channel_id=1, source_target_pairs={{1,0},{2,1},{3,2},{4,3},{5,4},{6,5},{7,6},{0,7},{9,8},{10,9},{11,1... | collective-permute-start | bytes 1179656 | tf_op jit(solution)/shard_map/ppermute | solution.py:17
  12.0 9.4 %collective-permute-start.2 = (s32[14,3]{1,0:T(8,128)S(1)}, s32[14,3]{1,0:T(8,128)S(1)}, u32[]{:S(2)}, u32[]{:S(2)}) collective-permute-start(s32[14,3]{1,0:T(8,128)S(1)} %get-tuple-element.27), channel_id=1, source_target_pairs={{0,8},{8,16},{16,24},{1,9},{9,17},{17,25},{2,10},{10,18},{18,26},{... | collective-permute-start | bytes 512 | tf_op jit(solution)/shard_map/ppermute | solution.py:16
  17.0 7.5 %collective-permute-start.10 = (f32[14,3]{1,0:T(8,128)S(1)}, f32[14,3]{1,0:T(8,128)S(1)}, u32[]{:S(2)}, u32[]{:S(2)}) collective-permute-start(f32[14,3]{1,0:T(8,128)S(1)} %get-tuple-element.25), channel_id=1, source_target_pairs={{0,8},{8,16},{16,24},{1,9},{9,17},{17,25},{2,10},{10,18},{18,26},{... | collective-permute-start | bytes 512 | tf_op jit(solution)/shard_map/ppermute | solution.py:16
  18.9 5.3 %collective-permute-start.3 = (s32[14,3]{1,0:T(8,128)S(1)}, s32[14,3]{1,0:T(8,128)S(1)}, u32[]{:S(2)}, u32[]{:S(2)}) collective-permute-start(s32[14,3]{1,0:T(8,128)S(1)} %get-tuple-element.28), channel_id=1, source_target_pairs={{8,0},{16,8},{24,16},{9,1},{17,9},{25,17},{10,2},{18,10},{26,18},{... | collective-permute-start | bytes 512 | tf_op jit(solution)/shard_map/ppermute | solution.py:17
  21.3 5.3 %collective-permute-start.11 = (f32[14,3]{1,0:T(8,128)S(1)}, f32[14,3]{1,0:T(8,128)S(1)}, u32[]{:S(2)}, u32[]{:S(2)}) collective-permute-start(f32[14,3]{1,0:T(8,128)S(1)} %get-tuple-element.26), channel_id=1, source_target_pairs={{8,0},{16,8},{24,16},{9,1},{17,9},{25,17},{10,2},{18,10},{26,18},{... | collective-permute-start | bytes 512 | tf_op jit(solution)/shard_map/ppermute | solution.py:17
  29.6 5.5 %collective-permute-start.6 = (f32[14,3,128]{2,1,0:T(4,128)S(1)}, f32[14,3,128]{2,1,0:T(4,128)S(1)}, u32[]{:S(2)}, u32[]{:S(2)}) collective-permute-start(f32[14,3,128]{2,1,0:T(4,128)S(1)} %get-tuple-element.7), channel_id=1, source_target_pairs={{0,8},{8,16},{16,24},{1,9},{9,17},{17,25},{2,10},{10,18},{18,26},{... | collective-permute-start | bytes 64520 | tf_op jit(solution)/shard_map/ppermute | solution.py:16
  33.2 5.2 %collective-permute-start.7 = (f32[14,3,128]{2,1,0:T(4,128)S(1)}, f32[14,3,128]{2,1,0:T(4,128)S(1)}, u32[]{:S(2)}, u32[]{:S(2)}) collective-permute-start(f32[14,3,128]{2,1,0:T(4,128)S(1)} %get-tuple-element.8), channel_id=1, source_target_pairs={{8,0},{16,8},{24,16},{9,1},{17,9},{25,17},{10,2},{18,10},{26,18},{... | collective-permute-start | bytes 64520 | tf_op jit(solution)/shard_map/ppermute | solution.py:17
  72.9 17.7 %collective-permute-start.12 = (f32[3,256,128]{2,1,0:T(8,128)S(1)}, f32[3,256,128]{2,1,0:T(8,128)S(1)}, u32[]{:S(2)}, u32[]{:S(2)}) collective-permute-start(f32[3,256,128]{2,1,0:T(8,128)S(1)} %get-tuple-element.9), channel_id=1, source_target_pairs={{0,1},{1,2},{2,3},{3,4},{4,5},{5,6},{6,7},{7,0},{8,9},{9,10},{10,1... | collective-permute-start | bytes 1179656 | tf_op jit(solution)/shard_map/ppermute | solution.py:16
  73.0 17.6 %collective-permute-start.13 = (f32[3,256,128]{2,1,0:T(8,128)S(1)}, f32[3,256,128]{2,1,0:T(8,128)S(1)}, u32[]{:S(2)}, u32[]{:S(2)}) collective-permute-start(f32[3,256,128]{2,1,0:T(8,128)S(1)} %get-tuple-element.10), channel_id=1, source_target_pairs={{1,0},{2,1},{3,2},{4,3},{5,4},{6,5},{7,6},{0,7},{9,8},{10,9},{11,1... | collective-permute-start | bytes 1179656 | tf_op jit(solution)/shard_map/ppermute | solution.py:17
  90.6 4.5 %collective-permute-start.14 = (f32[14,3,128]{2,1,0:T(4,128)S(1)}, f32[14,3,128]{2,1,0:T(4,128)S(1)}, u32[]{:S(2)}, u32[]{:S(2)}) collective-permute-start(f32[14,3,128]{2,1,0:T(4,128)S(1)} %get-tuple-element.5), channel_id=1, source_target_pairs={{0,8},{8,16},{16,24},{1,9},{9,17},{17,25},{2,10},{10,18},{18,26},{... | collective-permute-start | bytes 64520 | tf_op jit(solution)/shard_map/ppermute | solution.py:16
  92.6 5.2 %collective-permute-start.15 = (f32[14,3,128]{2,1,0:T(4,128)S(1)}, f32[14,3,128]{2,1,0:T(4,128)S(1)}, u32[]{:S(2)}, u32[]{:S(2)}) collective-permute-start(f32[14,3,128]{2,1,0:T(4,128)S(1)} %get-tuple-element.6), channel_id=1, source_target_pairs={{8,0},{16,8},{24,16},{9,1},{17,9},{25,17},{10,2},{18,10},{26,18},{... | collective-permute-start | bytes 64520 | tf_op jit(solution)/shard_map/ppermute | solution.py:17
where the time goes:
time: 136 us; the launch traced here: 133 us
  matrix products  69.6 us (51%)
  starting transfers between devices  31.7 us (23%)
  waiting for transfers between devices  27.3 us (20%)
  local copies, waits for them, and re-layouts  3.46 us (3%)
    dot_general x6, matrix products, vertical(): jnp.einsum('xyl,kml->xykm', values, inverses, precision=lax.Precision.HIG...  69.6 us
    ppermute x8, waiting for transfers between devices, with_halo(): before = lax.ppermute(last, axis, up)  18.4 us
    ppermute x8, starting transfers between devices, with_halo(): before = lax.ppermute(last, axis, up)  17.4 us
    ppermute x8, starting transfers between devices, with_halo(): after = lax.ppermute(initial, axis, down)  14.3 us
    ppermute x8, waiting for transfers between devices, with_halo(): after = lax.ppermute(initial, axis, down)  8.92 us
  transfers between devices with their start and end apart: 16, of which 6 were waited for; matrix products, arithmetic and copies ran while one was open for 2% of the time, Pallas kernels for 0%

commit v1 on v0

v1 whole, which is shorter than its diff:
```python
import functools

import jax
import jax.numpy as jnp
from jax import lax
from jax.experimental import pallas as pl
from jax.experimental.pallas import tpu as pltpu
from jax.sharding import PartitionSpec as P

STEPS = 6
EDGE = 8
PAD = 16
MESH = pl.DeviceIdType.MESH
F32 = jnp.float32
BF16 = jnp.bfloat16
AROUND = [(a, b) for a in (-1, 0, 1) for b in (-1, 0, 1) if (a, b) != (0, 0)]


def kernel(
    field, kappa, classes, inverses, out,
    u, neark, nearc, face_e, face_n, centre, parity, quad, weights,
    load_sem, send_k, recv_k, send_c, recv_c, send_e, recv_e, send_p, recv_p,
):
    nlon, nlat, lev = field.shape
    halo = STEPS
    span = nlon + 2 * halo
    low, high = PAD, PAD + nlat
    first, last = low - EDGE, high + EDGE
    rows = last - first
    lat, lon = lax.axis_index("lat"), lax.axis_index("lon")
    nlats, nlons = lax.axis_size("lat"), lax.axis_size("lon")
    has = {-1: lat > 0, 1: lat < nlats - 1}

    def device(dlat, dlon):
        return (lat + dlat, lax.rem(lon + dlon + nlons, nlons))

    loads = [
        pltpu.make_async_copy(
            field.at[j], u.at[0, halo + j, pl.ds(low, nlat)], load_sem.at[j]
        )
        for j in range(nlon)
    ]
    for load in loads:
        load.start()

    barrier = pltpu.get_barrier_semaphore()

    def guarded(dlat, action):
        if dlat == 0:
            action()
        else:
            pl.when(has[dlat])(action)

    for dlat in (-1, 0, 1):
        def greet(dlat=dlat):
            for a, b in AROUND:
                if a == dlat:
                    pl.semaphore_signal(
                        barrier, inc=1, device_id=device(a, b), device_id_type=MESH
                    )
        guarded(dlat, greet)
    peers = 2 + 3 * (has[-1].astype(jnp.int32) + has[1].astype(jnp.int32))
    pl.semaphore_wait(barrier, peers)

    small = []
    for n, (a, b) in enumerate(AROUND):
        for src, dst, ss, rs in (
            (kappa, neark, send_k, recv_k), (classes, nearc, send_c, recv_c)
        ):
            small.append((a, pltpu.make_async_remote_copy(
                src_ref=src, dst_ref=dst.at[1 - a, 1 - b],
                send_sem=ss.at[n], recv_sem=rs.at[n],
                device_id=device(a, b), device_id_type=MESH,
            )))
    lon_src = {-1: (halo, halo), 0: (halo, nlon), 1: (nlon, halo)}
    lon_dst = {-1: halo + nlon, 0: halo, 1: 0}
    edges = []
    for n, (a, b) in enumerate([ab for ab in AROUND if ab[0] != 0]):
        start, width = lon_src[b]
        edges.append((a, pltpu.make_async_remote_copy(
            src_ref=u.at[0, pl.ds(start, width), pl.ds(high - EDGE if a == 1 else low, EDGE)],
            dst_ref=u.at[0, pl.ds(lon_dst[b], width), pl.ds(first if a == 1 else high, EDGE)],
            send_sem=send_e.at[n], recv_sem=recv_e.at[n],
            device_id=device(a, b), device_id_type=MESH,
        )))
    planes = []
    for k in range(halo):
        for s, b in enumerate((1, -1)):
            src = halo + nlon - 1 - k if b == 1 else halo + k
            dst = halo - 1 - k if b == 1 else halo + nlon + k
            planes.append(pltpu.make_async_remote_copy(
                src_ref=u.at[0, src, pl.ds(low, nlat)],
                dst_ref=u.at[0, dst, pl.ds(low, nlat)],
                send_sem=send_p.at[2 * k + s], recv_sem=recv_p.at[2 * k + s],
                device_id=device(0, b), device_id_type=MESH,
            ))

    def start_all(group):
        for dlat in (0, -1, 1):
            def go(dlat=dlat):
                for a, copy in group:
                    if a == dlat:
                        copy.start()
            guarded(dlat, go)

    start_all(small)
    for load in loads:
        load.wait()
    start_all(edges)
    for copy in planes:
        copy.start()

    kinds = inverses.shape[0]
    for c in range(kinds):
        w = jnp.transpose(inverses[c])
        wh = w.astype(BF16)
        wl = (w - wh.astype(F32)).astype(BF16)
        r, q = (c % 2) * lev, (c // 2) * lev
        weights[pl.ds(r, lev), pl.ds(q, lev)] = wh
        weights[pl.ds(2 * lev + r, lev), pl.ds(q, lev)] = wh
        weights[pl.ds(4 * lev + r, lev), pl.ds(q, lev)] = wl

    for a in (-1, 1):
        @pl.when(jnp.logical_not(has[a]))
        def _(a=a):
            for b in range(3):
                neark[1 + a, b] = jnp.zeros((nlon, nlat), F32)
                nearc[1 + a, b] = jnp.zeros((nlon, nlat), jnp.int32)
            edge = first if a == -1 else high
            u[0, :, pl.ds(edge, EDGE)] = jnp.zeros((span, EDGE, lev), F32)

    def wait_all(group):
        for dlat in (0, -1, 1):
            def go(dlat=dlat):
                for a, copy in group:
                    if -a == dlat:
                        copy.wait_recv()
            guarded(dlat, go)

    wait_all(small)
    neark[1, 1] = kappa[...]
    nearc[1, 1] = classes[...]

    def turned(near):
        strips = []
        for b in range(3):
            strips.append(jnp.concatenate(
                [near[0, b][:, nlat - 128:], near[1, b], near[2, b][:, :128]], axis=1
            ).astype(F32))
        lines = jnp.concatenate(
            strips + [jnp.zeros((128 - 3 * nlon, nlat + 256), F32)], axis=0
        )
        tall = jnp.concatenate(
            [jnp.transpose(lines[:, g:g + 128]) for g in range(0, nlat + 256, 128)], axis=0
        )
        return tall[128 - PAD:128 + nlat + PAD]

    kt = turned(neark)
    ct = turned(nearc)
    total = nlat + 2 * PAD
    at = lat * nlat - PAD + lax.broadcasted_iota(jnp.int32, (total, 128), 0)
    inside = jnp.where((at >= 0) & (at < nlat * nlats), 1.0, 0.0).astype(F32)
    ke = 0.5 * (kt + pltpu.roll(kt, 127, 1))
    kw = pltpu.roll(ke, 1, 1)
    kn = 0.5 * (kt + pltpu.roll(kt, total - 1, 0))
    ks = pltpu.roll(kn, 1, 0)
    c0 = (1.0 - (ke + kw + kn + ks)) * inside
    fe = ke * inside
    fn = kn * inside * pltpu.roll(inside, total - 1, 0)
    half = jnp.floor(ct * 0.5)
    odd = ct - 2.0 * half
    shift = nlon - halo
    for p in range(span):
        def wide(x):
            return jnp.broadcast_to(x[:, p + shift:p + shift + 1], (total, lev))
        face_e[p] = wide(fe)
        face_n[p] = wide(fn)
        centre[p] = wide(c0)
        quad[p] = wide(half)
        parity[p] = wide(odd)[first:last].astype(BF16)

    wait_all(edges)

    mid = pl.ds(first, rows)
    up = pl.ds(first + 1, rows)
    down = pl.ds(first - 1, rows)

    def pair(t, i):
        sides = (i, span - 1 - i)
        lhs = []
        for p in sides:
            v = centre[p, mid] * u[t - 1, p, mid]
            v = v + face_e[p, mid] * u[t - 1, p + 1, mid]
            v = v + face_e[p - 1, mid] * u[t - 1, p - 1, mid]
            v = v + face_n[p, mid] * u[t - 1, p, up]
            v = v + face_n[p, down] * u[t - 1, p, down]
            vh = v.astype(BF16)
            vl = (v - vh.astype(F32)).astype(BF16)
            odds = parity[p]
            ho = vh * odds
            he = vh - ho
            lo = vl * odds
            le = vl - lo
            lhs.append(jnp.concatenate([he, ho, le, lo, he, ho], axis=1))
        res = jnp.dot(
            jnp.concatenate(lhs, axis=0), weights[...], preferred_element_type=F32
        )
        for n, p in enumerate(sides):
            r = res[n * rows:(n + 1) * rows]
            kind = quad[p, mid]
            pick = r[:, :lev]
            for q in range(1, kinds // 2):
                pick = jnp.where(kind == float(q), r[:, q * lev:(q + 1) * lev], pick)
            u[t, p, mid] = pick

    def finish(i):
        for p in (i, span - 1 - i):
            out[p - halo] = u[STEPS, p, pl.ds(low, nlat)]

    for t in range(1, STEPS + 1):
        def inner(i, carry, t=t):
            pair(t, i)
            return carry
        if halo + t < span // 2:
            lax.fori_loop(halo + t, span // 2, inner, 0)
    for k in range(1, halo + 1):
        planes[2 * k - 2].wait_recv()
        planes[2 * k - 1].wait_recv()
        top = min(STEPS, span // 2 - 1 - halo + k)

        def wave(t, carry, k=k):
            pair(t, halo - k + t)
            return carry
        lax.fori_loop(1, top + 1, wave, 0)
        if top == STEPS:
            finish(halo - k + STEPS)

    for group in (small, edges):
        for dlat in (0, -1, 1):
            def done(dlat=dlat, group=group):
                for a, copy in group:
                    if a == dlat:
                        copy.wait_send()
            guarded(dlat, done)
    for copy in planes:
        copy.wait_send()


def body(field, kappa, classes, inverses):
    nlon, nlat, lev = field.shape
    span = nlon + 2 * STEPS
    total = nlat + 2 * PAD
    kinds = inverses.shape[0]
    vmem = pl.BlockSpec(memory_space=pltpu.VMEM)
    dma = pltpu.SemaphoreType.DMA
    return pl.pallas_call(
        kernel,
        out_shape=jax.ShapeDtypeStruct(field.shape, F32),
        in_specs=[pl.BlockSpec(memory_space=pl.ANY), vmem, vmem, vmem],
        out_specs=vmem,
        scratch_shapes=[
            pltpu.VMEM((STEPS + 1, span, total, lev), F32),
            pltpu.VMEM((3, 3, nlon, nlat), F32),
            pltpu.VMEM((3, 3, nlon, nlat), jnp.int32),
            pltpu.VMEM((span, total, lev), F32),
            pltpu.VMEM((span, total, lev), F32),
            pltpu.VMEM((span, total, lev), F32),
            pltpu.VMEM((span, total - 2 * (PAD - EDGE), lev), BF16),
            pltpu.VMEM((span, total, lev), F32),
            pltpu.VMEM((6 * lev, kinds // 2 * lev), BF16),
            dma((nlon,)), dma((8,)), dma((8,)), dma((8,)), dma((8,)),
            dma((6,)), dma((6,)), dma((2 * STEPS,)), dma((2 * STEPS,)),
        ],
        compiler_params=pltpu.CompilerParams(
            collective_id=0, has_side_effects=True, vmem_limit_bytes=60 * 1024 * 1024
        ),
    )(field, kappa, classes, inverses)


def solution(mesh):
    return jax.shard_map(
        body,
        mesh=mesh,
        in_specs=(P("lon", "lat", None), P("lon", "lat"), P("lon", "lat"), P()),
        out_specs=P("lon", "lat", None),
        check_vma=False,
    )
```

time: 136 us -> 58 us (0.43); the launches traced: 133 us -> 57.9 us
  matrix products: 69.6 us -> 0 us
  Pallas kernels: 0 us -> 55.6 us
  starting transfers between devices: 31.7 us -> 0 us
  waiting for transfers between devices: 27.3 us -> 0 us
    dot_general x6 -> x0, matrix products: 69.6 us -> none  [vertical(): jnp.einsum('xyl,kml->xykm', values, inverses, precision=lax.Precision.HIG...]
    pallas_call x0 -> x1, Pallas kernels: none -> 55.6 us  [body(): pl.pallas_call(kernel, out_shape=jax.ShapeDtypeStruct(field.shape, F32),...]
    ppermute x16 -> x0, starting transfers between devices: 31.7 us -> none  [the longest x8 17.4 us: with_halo(): before = lax.ppermute(last, axis, up)]
    ppermute x16 -> x0, waiting for transfers between devices: 27.3 us -> none  [the longest x8 18.4 us: with_halo(): before = lax.ppermute(last, axis, up)]
    slice x12 -> x0, local copies, waits for them, and re-layouts: 3.32 us -> none  [the longest x6 1.79 us: with_halo(): last = lax.slice_in_dim(array, length - width, length, axis=dim)]
    unnamed x10 -> x1, local copies, waits for them, and re-layouts: 0.12 us -> 2.27 us
  transfers between devices with their start and end apart: 16 -> 0, of which waited for: 6 -> 0; matrix products, arithmetic and copies ran while one was open for 2% -> 0% of each run, Pallas kernels for 0% -> 0%
where the time goes in v1:
time: 58 us; the launch traced here: 57.9 us
  Pallas kernels  55.6 us (96%)
  local copies, waits for them, and re-layouts  2.27 us (4%)
    pallas_call x1, Pallas kernels, body(): pl.pallas_call(kernel, out_shape=jax.ShapeDtypeStruct(field.shape, F32),...  55.6 us
    unnamed x1, local copies, waits for them, and re-layouts  2.27 us

profile of v1, /device:TPU:3, one launch (start us, length us, event | category | flops | bytes accessed | tf_op | source)
XLA Modules:
  0.0 57.9 jit_solution(2783880196560129790)
XLA Ops:
  0.0 55.6 %shard_map.46 = f32[8,256,128]{2,1,0:T(8,128)} custom-call(f32[8,256,128]{2,1,0:T(8,128)} %field.1, f32[8,256]{1,0:T(8,128)} %kappa.1, s32[8,256]{1,0:T(8,128)} %classes.1, f32[8,128,128]{2,1,0:T(8,128)} %inverses.1), custom_call_target="tpu_custom_call" | custom-call | tf_op jit(solution)/shard_map/pallas_call | solution.py:256
  55.6 2.3 %copy.6 = f32[8,256,128]{2,1,0:T(8,128)} copy(f32[8,256,128]{2,1,0:T(8,128)} %shard_map.46) | data formatting | bytes 2097152

commit v2 on v1

v2 whole, which is shorter than its diff:
```python
import functools

import jax
import jax.numpy as jnp
from jax import lax
from jax.experimental import pallas as pl
from jax.experimental.pallas import tpu as pltpu
from jax.sharding import PartitionSpec as P

STEPS = 6
EDGE = 8
PAD = 16
MESH = pl.DeviceIdType.MESH
F32 = jnp.float32
BF16 = jnp.bfloat16


def kernel(
    field, kappa, classes, inverses, out,
    u, mine, final, neark, nearc, face_e, face_n, centre, parity, quad, weights,
    load_sem, own_sem, store_sem, send_k, recv_k, send_c, recv_c,
    send_e, recv_e, send_p, recv_p,
):
    nlon, nlat, lev = field.shape
    halo = STEPS
    span = 2 * (nlon + halo)
    half = nlat // 2
    total = half + 2 * PAD
    low, high = PAD, PAD + half
    first, last = low - EDGE, high + EDGE
    rows = last - first
    main = half + EDGE
    lat, lon = lax.axis_index("lat"), lax.axis_index("lon")
    nlats, nlons = lax.axis_size("lat"), lax.axis_size("lon")
    s = lax.rem(lon, 2)
    g = 1 - 2 * s
    d = -g
    has_out = jnp.logical_and(lat + d >= 0, lat + d < nlats)
    has_in = jnp.logical_and(lat - d >= 0, lat - d < nlats)

    def device(dlat, dlon):
        return (lat + dlat, lax.rem(lon + dlon + nlons, nlons))

    def place(n):
        return (nlon - 1) * s + g * n

    def main_src(q):
        return pl.multiple_of((half - EDGE) * q, EDGE)

    def main_dst(q):
        return pl.multiple_of(low - EDGE * q, EDGE)

    def outer_src(q):
        return pl.multiple_of((nlat - EDGE) * (1 - q), EDGE)

    def outer_dst(q):
        return pl.multiple_of(first + main * q, EDGE)

    order = list(range(nlon))[::-1]
    loads = {}
    for n in order:
        loads[n] = pltpu.make_async_copy(field.at[place(n)], mine.at[n], load_sem.at[n])
        loads[n].start()
    owns = [
        pltpu.make_async_copy(
            field.at[place(n), pl.ds(main_src(s), main)],
            u.at[0, halo + n, pl.ds(main_dst(s), main)],
            own_sem.at[n],
        )
        for n in range(nlon)
    ]
    for copy in owns:
        copy.start()

    barrier = pltpu.get_barrier_semaphore()

    def greet(dlat, dlons):
        for dlon in dlons:
            pl.semaphore_signal(
                barrier, inc=1, device_id=device(dlat, dlon), device_id_type=MESH
            )

    greet(0, (g, -g, 2 * g, -2 * g))

    @pl.when(has_in)
    def _():
        greet(-d, (0, -2 * g))

    @pl.when(has_out)
    def _():
        greet(d, (0, g, -g, 2 * g))

    pl.semaphore_wait(
        barrier, 4 + 2 * has_in.astype(jnp.int32) + 4 * has_out.astype(jnp.int32)
    )

    targets = [
        (0, g, 0, 2), (0, -g, 0, 0), (0, -2 * g, 0, 3),
        (-d, 0, 1, 1), (-d, -2 * g, 1, 3),
        (d, g, 1, 2), (d, -g, 1, 0),
    ]
    small = []
    for n, (a, b, outer, slot) in enumerate(targets):
        for src, dst, ss, rs in (
            (kappa, neark, send_k, recv_k), (classes, nearc, send_c, recv_c)
        ):
            small.append(pltpu.make_async_remote_copy(
                src_ref=src, dst_ref=dst.at[outer, slot],
                send_sem=ss.at[n], recv_sem=rs.at[n],
                device_id=device(a, b), device_id_type=MESH,
            ))
    small_near, small_in, small_out = small[:6], small[6:10], small[10:]

    edge_count = [0]

    def edge(src, dst, q, a, b):
        n = edge_count[0]
        edge_count[0] += 1
        return pltpu.make_async_remote_copy(
            src_ref=src.at[:, pl.ds(outer_src(q), EDGE)],
            dst_ref=dst.at[:, pl.ds(outer_dst(q), EDGE)],
            send_sem=send_e.at[n], recv_sem=recv_e.at[n],
            device_id=device(a, b), device_id_type=MESH,
        )

    begin = u.at[0]
    edges_in = [
        edge(mine, begin.at[pl.ds(halo, nlon)], s, -d, 0),
        edge(mine.at[pl.ds(0, halo)], begin.at[pl.ds(halo + 2 * nlon, halo)], s, -d, -2 * g),
    ]
    edges_out = [
        edge(mine.at[pl.ds(n, 1)], begin.at[pl.ds(span - 1 - halo - n, 1)], 1 - s, d, g)
        for n in range(nlon)
    ] + [
        edge(mine.at[pl.ds(n, 1)], begin.at[pl.ds(halo - 1 - n, 1)], 1 - s, d, -g)
        for n in range(halo)
    ]

    def plane(n, src, dst, b):
        return pltpu.make_async_remote_copy(
            src_ref=src, dst_ref=dst, send_sem=send_p.at[n], recv_sem=recv_p.at[n],
            device_id=device(0, b), device_id_type=MESH,
        )

    swaps = [
        plane(
            n,
            mine.at[nlon - 1 - n, pl.ds(main_src(1 - s), main)],
            u.at[0, halo + nlon + n, pl.ds(main_dst(1 - s), main)],
            g,
        )
        for n in range(nlon)
    ]
    direct = [
        plane(
            nlon + n,
            mine.at[n, pl.ds(main_src(s), main)],
            u.at[0, halo + 2 * nlon + n, pl.ds(main_dst(s), main)],
            -2 * g,
        )
        for n in range(halo)
    ]
    relays = [
        plane(
            nlon + halo + n,
            u.at[0, 2 * nlon + n, pl.ds(main_dst(s), main)],
            u.at[0, n, pl.ds(main_dst(s), main)],
            2 * g,
        )
        for n in range(halo)
    ]
    returns = [
        plane(
            nlon + 2 * halo + n,
            u.at[STEPS, halo + nlon + n, pl.ds(low, half)],
            final.at[nlon - 1 - n],
            g,
        )
        for n in range(nlon)
    ]

    for copy in small_near:
        copy.start()

    @pl.when(has_in)
    def _():
        for copy in small_in:
            copy.start()

    @pl.when(has_out)
    def _():
        for copy in small_out:
            copy.start()

    for n in order:
        loads[n].wait()
        swaps[nlon - 1 - n].start()
    for copy in direct:
        copy.start()

    @pl.when(has_in)
    def _():
        for copy in edges_in:
            copy.start()

    @pl.when(has_out)
    def _():
        for copy in edges_out:
            copy.start()

    kinds = inverses.shape[0]
    for c in range(kinds):
        w = jnp.transpose(inverses[c])
        wh = w.astype(BF16)
        wl = (w - wh.astype(F32)).astype(BF16)
        r, q = (c % 2) * lev, (c // 2) * lev
        weights[pl.ds(r, lev), pl.ds(q, lev)] = wh
        weights[pl.ds(2 * lev + r, lev), pl.ds(q, lev)] = wh
        weights[pl.ds(4 * lev + r, lev), pl.ds(q, lev)] = wl

    @pl.when(jnp.logical_not(has_out))
    def _():
        for slot in range(4):
            neark[1, slot] = jnp.zeros((nlon, nlat), F32)
            nearc[1, slot] = jnp.zeros((nlon, nlat), jnp.int32)
        u[0, :, pl.ds(outer_dst(s), EDGE)] = jnp.zeros((span, EDGE, lev), F32)

    neark[0, 1] = kappa[...]
    nearc[0, 1] = classes[...]
    for copy in small_near:
        copy.wait_recv()

    @pl.when(has_out)
    def _():
        for copy in small_in + small_out:
            copy.wait_recv()

    upright = s == 0

    def turned(near):
        strips = []
        for slot in range(4):
            here, there = near[0, slot].astype(F32), near[1, slot].astype(F32)
            line = jnp.where(
                upright,
                jnp.concatenate([there[:, nlat - 128:], here[:, :half + 128]], axis=1),
                jnp.concatenate([here[:, half - 128:], there[:, :128]], axis=1),
            )
            back = jnp.concatenate([line[n:n + 1] for n in range(nlon)[::-1]], axis=0)
            strips.append(jnp.where(upright, line, back))
        lines = jnp.concatenate(
            strips + [jnp.zeros((128 - 4 * nlon, half + 256), F32)], axis=0
        )
        tall = jnp.concatenate(
            [jnp.transpose(lines[:, c:c + 128]) for c in range(0, half + 256, 128)], axis=0
        )
        return tall[128 - PAD:128 + half + PAD]

    kt = turned(neark)
    ct = turned(nearc)
    at = lat * nlat + half * s - PAD + lax.broadcasted_iota(jnp.int32, (total, 128), 0)
    inside = jnp.where((at >= 0) & (at < nlat * nlats), 1.0, 0.0).astype(F32)
    ke = 0.5 * (kt + pltpu.roll(kt, 127, 1))
    kw = pltpu.roll(ke, 1, 1)
    kn = 0.5 * (kt + pltpu.roll(kt, total - 1, 0))
    ks = pltpu.roll(kn, 1, 0)
    c0 = (1.0 - (ke + kw + kn + ks)) * inside
    fe = ke * inside
    fn = kn * inside * pltpu.roll(inside, total - 1, 0)
    whole = jnp.floor(ct * 0.5)
    odd = ct - 2.0 * whole
    shift = nlon - halo
    for p in range(span):
        def wide(x):
            return jnp.broadcast_to(x[:, p + shift:p + shift + 1], (total, lev))
        face_e[p] = wide(fe)
        face_n[p] = wide(fn)
        centre[p] = wide(c0)
        quad[p] = wide(whole)
        parity[p] = wide(odd)[first:last].astype(BF16)

    for copy in owns:
        copy.wait()

    @pl.when(has_out)
    def _():
        for copy in edges_in + edges_out:
            copy.wait_recv()

    mid = pl.ds(first, rows)
    up = pl.ds(first + 1, rows)
    down = pl.ds(first - 1, rows)

    def pair(t, i):
        sides = (i, i + 1)
        lhs = []
        for p in sides:
            v = centre[p, mid] * u[t - 1, p, mid]
            v = v + face_e[p, mid] * u[t - 1, p + 1, mid]
            v = v + face_e[p - 1, mid] * u[t - 1, p - 1, mid]
            v = v + face_n[p, mid] * u[t - 1, p, up]
            v = v + face_n[p, down] * u[t - 1, p, down]
            vh = v.astype(BF16)
            vl = (v - vh.astype(F32)).astype(BF16)
            odds = parity[p]
            ho = vh * odds
            he = vh - ho
            lo = vl * odds
            le = vl - lo
            lhs.append(jnp.concatenate([he, ho, le, lo, he, ho], axis=1))
        res = jnp.dot(
            jnp.concatenate(lhs, axis=0), weights[...], preferred_element_type=F32
        )
        for n, p in enumerate(sides):
            r = res[n * rows:(n + 1) * rows]
            kind = quad[p, mid]
            pick = r[:, :lev]
            for q in range(1, kinds // 2):
                pick = jnp.where(kind == float(q), r[:, q * lev:(q + 1) * lev], pick)
            u[t, p, mid] = pick

    def store(n):
        return pltpu.make_async_copy(
            u.at[STEPS, halo + n, pl.ds(low, half)],
            out.at[place(n), pl.ds(pl.multiple_of(half * s, EDGE), half)],
            store_sem.at[n],
        )

    for t in range(1, STEPS + 1):
        def inner(i, carry, t=t):
            pair(t, halo + t + 2 * i)
            return carry
        count = nlon // 2 - t
        if count > 0:
            lax.fori_loop(0, count, inner, 0)

    def done(p):
        if halo <= p < halo + nlon:
            store(p - halo).start()
        elif halo + nlon <= p < halo + 2 * nlon:
            returns[p - halo - nlon].start()

    for b in range(halo + nlon, span, 2):
        for p in (b, b + 1):
            if p < halo + 2 * nlon:
                swaps[p - halo - nlon].wait_recv()
                if p >= 2 * nlon:
                    relays[p - 2 * nlon].start()
            else:
                direct[p - halo - 2 * nlon].wait_recv()
        top = min(STEPS, (b - halo) // 2)

        def wave(t, carry, b=b):
            pair(t, b - t)
            return carry
        lax.fori_loop(1, top + 1, wave, 0)
        if top == STEPS:
            done(b - STEPS)
            done(b + 1 - STEPS)
    for a in range(halo - 2, -1, -2):
        relays[a + 1].wait_recv()
        relays[a].wait_recv()

        def wave_left(t, carry, a=a):
            pair(t, a + t)
            return carry
        lax.fori_loop(1, STEPS + 1, wave_left, 0)
        done(a + STEPS)
        done(a + 1 + STEPS)

    def store_back(n):
        return pltpu.make_async_copy(
            final.at[n],
            out.at[place(n), pl.ds(pl.multiple_of(half * (1 - s), EDGE), half)],
            store_sem.at[nlon + n],
        )

    for n in range(nlon):
        returns[n].wait_recv()
        store_back(nlon - 1 - n).start()

    for copy in small_near + swaps + direct + relays + returns:
        copy.wait_send()

    @pl.when(has_in)
    def _():
        for copy in small_in + edges_in:
            copy.wait_send()

    @pl.when(has_out)
    def _():
        for copy in small_out + edges_out:
            copy.wait_send()

    for n in range(nlon):
        store(n).wait()
        store_back(n).wait()


def body(field, kappa, classes, inverses):
    nlon, nlat, lev = field.shape
    span = 2 * (nlon + STEPS)
    half = nlat // 2
    total = half + 2 * PAD
    kinds = inverses.shape[0]
    vmem = pl.BlockSpec(memory_space=pltpu.VMEM)
    anywhere = pl.BlockSpec(memory_space=pl.ANY)
    dma = pltpu.SemaphoreType.DMA
    planes = 2 * nlon + 2 * STEPS
    edges = 2 + nlon + STEPS
    return pl.pallas_call(
        kernel,
        out_shape=jax.ShapeDtypeStruct(field.shape, F32),
        in_specs=[anywhere, vmem, vmem, vmem],
        out_specs=anywhere,
        scratch_shapes=[
            pltpu.VMEM((STEPS + 1, span, total, lev), F32),
            pltpu.VMEM((nlon, nlat, lev), F32),
            pltpu.VMEM((nlon, half, lev), F32),
            pltpu.VMEM((2, 4, nlon, nlat), F32),
            pltpu.VMEM((2, 4, nlon, nlat), jnp.int32),
            pltpu.VMEM((span, total, lev), F32),
            pltpu.VMEM((span, total, lev), F32),
            pltpu.VMEM((span, total, lev), F32),
            pltpu.VMEM((span, total - 2 * (PAD - EDGE), lev), BF16),
            pltpu.VMEM((span, total, lev), F32),
            pltpu.VMEM((6 * lev, kinds // 2 * lev), BF16),
            dma((nlon,)), dma((nlon,)), dma((2 * nlon,)),
            dma((7,)), dma((7,)), dma((7,)), dma((7,)),
            dma((edges,)), dma((edges,)), dma((planes,)), dma((planes,)),
        ],
        compiler_params=pltpu.CompilerParams(
            collective_id=0, has_side_effects=True, vmem_limit_bytes=60 * 1024 * 1024
        ),
    )(field, kappa, classes, inverses)


def solution(mesh):
    return jax.shard_map(
        body,
        mesh=mesh,
        in_specs=(P("lon", "lat", None), P("lon", "lat"), P("lon", "lat"), P()),
        out_specs=P("lon", "lat", None),
        check_vma=False,
    )
```

time: 58 us -> 53.5 us (0.922)
  the two profiles are of different devices: /device:TPU:3 before, /device:TPU:1 now
where the time goes in v2:
time: 53.5 us; the launch traced here: 53.4 us
  Pallas kernels  51.1 us (96%)
  local copies, waits for them, and re-layouts  2.27 us (4%)
    pallas_call x1, Pallas kernels, body(): pl.pallas_call(kernel, out_shape=jax.ShapeDtypeStruct(field.shape, F32),...  51.1 us
    unnamed x1, local copies, waits for them, and re-layouts  2.27 us

profile of v2, /device:TPU:1, one launch (start us, length us, event | category | flops | bytes accessed | tf_op | source)
XLA Modules:
  0.0 53.4 jit_solution(1659765995187441287)
XLA Ops:
  0.0 51.1 %shard_map.46 = f32[8,256,128]{2,1,0:T(8,128)} custom-call(f32[8,256,128]{2,1,0:T(8,128)} %field.1, f32[8,256]{1,0:T(8,128)} %kappa.1, s32[8,256]{1,0:T(8,128)} %classes.1, f32[8,128,128]{2,1,0:T(8,128)} %inverses.1), custom_call_target="tpu_custom_call" | custom-call | tf_op jit(solution)/shard_map/pallas_call | solution.py:411
  51.1 2.3 %copy.6 = f32[8,256,128]{2,1,0:T(8,128)} copy(f32[8,256,128]{2,1,0:T(8,128)} %shard_map.46) | data formatting | bytes 2097152

commit v3 on v2

--- a/solution.py
+++ b/solution.py
@@ -194,9 +194,6 @@
 
     for n in order:
         loads[n].wait()
-        swaps[nlon - 1 - n].start()
-    for copy in direct:
-        copy.start()
 
     @pl.when(has_in)
     def _():
@@ -207,6 +204,9 @@
     def _():
         for copy in edges_out:
             copy.start()
+
+    for copy in swaps + direct:
+        copy.start()
 
     kinds = inverses.shape[0]
     for c in range(kinds):
@@ -284,15 +284,13 @@
 
     @pl.when(has_out)
     def _():
-        for copy in edges_in + edges_out:
-            copy.wait_recv()
+        edges_in[0].wait_recv()
 
     mid = pl.ds(first, rows)
     up = pl.ds(first + 1, rows)
     down = pl.ds(first - 1, rows)
 
-    def pair(t, i):
-        sides = (i, i + 1)
+    def columns(t, sides):
         lhs = []
         for p in sides:
             v = centre[p, mid] * u[t - 1, p, mid]
@@ -328,11 +326,16 @@
 
     for t in range(1, STEPS + 1):
         def inner(i, carry, t=t):
-            pair(t, halo + t + 2 * i)
+            columns(t, (halo + t + 2 * i, halo + t + 2 * i + 1))
             return carry
         count = nlon // 2 - t
         if count > 0:
             lax.fori_loop(0, count, inner, 0)
+
+    @pl.when(has_out)
+    def _():
+        for copy in edges_in[1:] + edges_out:
+            copy.wait_recv()
 
     def done(p):
         if halo <= p < halo + nlon:
@@ -340,33 +343,41 @@
         elif halo + nlon <= p < halo + 2 * nlon:
             returns[p - halo - nlon].start()
 
-    for b in range(halo + nlon, span, 2):
-        for p in (b, b + 1):
-            if p < halo + 2 * nlon:
-                swaps[p - halo - nlon].wait_recv()
-                if p >= 2 * nlon:
-                    relays[p - 2 * nlon].start()
-            else:
-                direct[p - halo - 2 * nlon].wait_recv()
-        top = min(STEPS, (b - halo) // 2)
-
-        def wave(t, carry, b=b):
-            pair(t, b - t)
+    def arrive(p):
+        if p < halo:
+            relays[p].wait_recv()
+        elif p < halo + 2 * nlon:
+            swaps[p - halo - nlon].wait_recv()
+            if p >= 2 * nlon:
+                relays[p - 2 * nlon].start()
+        else:
+            direct[p - halo - 2 * nlon].wait_recv()
+
+    right = list(range(halo + nlon, span))
+    left = list(range(halo))[::-1]
+    cut = STEPS - nlon // 2
+    waves = [(right[2 * n:2 * n + 2], []) for n in range(cut)]
+    rest = right[2 * cut:]
+    while len(rest) >= 4:
+        waves.append((rest[:4], []))
+        rest = rest[4:]
+    waves.append((rest, left[:4 - len(rest)]))
+    left = left[4 - len(rest):]
+    while left:
+        waves.append(([], left[:4]))
+        left = left[4:]
+    for east, west in waves:
+        for p in east + west:
+            arrive(p)
+        top = min([STEPS] + [(p - halo) // 2 for p in east])
+
+        def wave(t, carry, east=east, west=west):
+            columns(t, [p - t for p in east] + [p + t for p in west])
             return carry
         lax.fori_loop(1, top + 1, wave, 0)
         if top == STEPS:
-            done(b - STEPS)
-            done(b + 1 - STEPS)
-    for a in range(halo - 2, -1, -2):
-        relays[a + 1].wait_recv()
-        relays[a].wait_recv()
-
-        def wave_left(t, carry, a=a):
-            pair(t, a + t)
-            return carry
-        lax.fori_loop(1, STEPS + 1, wave_left, 0)
-        done(a + STEPS)
-        done(a + 1 + STEPS)
+            for p in [p - STEPS for p in east] + [p + STEPS for p in west]:
+                done(p)
 
     def store_back(n):
         return pltpu.make_async_copy(

time: 53.5 us -> 44.6 us (0.83)
  the two profiles are of different devices: /device:TPU:1 before, /device:TPU:3 now
where the time goes in v3:
time: 44.6 us; the launch traced here: 44.1 us
  Pallas kernels  41.8 us (94%)
  local copies, waits for them, and re-layouts  2.27 us (5%)
    pallas_call x1, Pallas kernels, body(): pl.pallas_call(kernel, out_shape=jax.ShapeDtypeStruct(field.shape, F32),...  41.8 us
    unnamed x1, local copies, waits for them, and re-layouts  2.27 us

profile of v3, /device:TPU:3, one launch (start us, length us, event | category | flops | bytes accessed | tf_op | source)
XLA Modules:
  0.0 44.1 jit_solution(6118637793114534328)
XLA Ops:
  0.0 41.8 %shard_map.46 = f32[8,256,128]{2,1,0:T(8,128)} custom-call(f32[8,256,128]{2,1,0:T(8,128)} %field.1, f32[8,256]{1,0:T(8,128)} %kappa.1, s32[8,256]{1,0:T(8,128)} %classes.1, f32[8,128,128]{2,1,0:T(8,128)} %inverses.1), custom_call_target="tpu_custom_call" | custom-call | tf_op jit(solution)/shard_map/pallas_call | solution.py:422
  41.9 2.3 %copy.6 = f32[8,256,128]{2,1,0:T(8,128)} copy(f32[8,256,128]{2,1,0:T(8,128)} %shard_map.46) | data formatting | bytes 2097152
